TPU v7x, 32 devices: a whole 2x2x4 slice. The times are simulated.
32 devices in a mesh: dp: 4 (over z), fsdp: 8 (over y, x, core).
Axes of the slice: x: 2, y: 2, z: 4, core: 2. Of those that a mesh axis runs over, the one named last changes fastest.
Arguments:
- hidden: bfloat16 [8192, 4096], P(('dp', 'fsdp')), may hold values from -6 to 6
- queries: bfloat16 [8192, 2048], P(('dp', 'fsdp')), may hold values from -6 to 6
- keys: bfloat16 [8192, 512], P(('dp', 'fsdp')), may hold values from -6 to 6
- target: bfloat16 [8192, 2048], P(('dp', 'fsdp')), may hold values from -6 to 6
- lengths: int32 [32], P(('dp', 'fsdp')), may hold values from 64 to 256
- value_weight_frozen: bfloat16 [4096, 512], P('fsdp'), may hold values from -0.09375 to 0.09375
- adapter_down_map: float32 [4096, 64], P('fsdp'), may hold values from -0.09375 to 0.09375
- adapter_up_map: float32 [64, 512], replicated, may hold values from -0.75 to 0.75
- average_down_map: float32 [4096, 64], P('fsdp'), may hold values from -0.09375 to 0.09375
- average_up_map: float32 [64, 512], replicated, may hold values from -0.75 to 0.75
Outputs:
- down_map_gradient: float32 [4096, 64], P('fsdp')
- up_map_gradient: float32 [64, 512], replicated
- average_down_next: float32 [4096, 64], P('fsdp')
- average_up_next: float32 [64, 512], replicated
- loss: float32 [], replicated
Inputs may be any that keep to these rules, and one draw needn't show every extreme that they name: `lengths`: slots at or past a sequence's length are padding.
All inputs are finite; a program needn't handle non-finite values.
Results may differ from a plain program's by a relative error of at most 0.0049.
Values may be sent and summed in bfloat16 or wider, within the bound.
A program may use at most 64 MiB of HBM per device.

v0:
```python
import math

import jax
import jax.numpy as jnp
from jax import lax
from jax.sharding import PartitionSpec as P

HEADS = 16
KEY_VALUE_HEADS = 4
HEAD_DIM = 128


adapter_scale = 2.0
average_decay = 0.9
learning_rate = 1.0
masked_score = -1e30


def per_device(
    hidden,
    queries,
    keys,
    target,
    lengths,
    value_weight_frozen,
    adapter_down_map,
    adapter_up_map,
    average_down_map,
    average_up_map,
):
    tok_rows = hidden.shape[0]
    group_size = HEADS // KEY_VALUE_HEADS
    seq_length = lengths[0]
    down_factor_slice = adapter_down_map.astype(jnp.bfloat16)
    up_factor_slice = adapter_up_map.astype(jnp.bfloat16)
    columns = hidden
    frozen_value_output = jnp.dot(
        columns,
        lax.all_gather(value_weight_frozen, "fsdp", axis=0, tiled=True),
        preferred_element_type=jnp.float32,
    )
    adapter_hidden = jnp.dot(
        columns,
        lax.all_gather(down_factor_slice, "fsdp", axis=0, tiled=True),
        preferred_element_type=jnp.float32,
    )
    adapter_hidden = adapter_hidden.astype(jnp.bfloat16)
    value_outputs = (
        frozen_value_output
        + adapter_scale
        * jnp.dot(adapter_hidden, up_factor_slice, preferred_element_type=jnp.float32)
    ).astype(jnp.bfloat16)
    position = jnp.arange(tok_rows, dtype=jnp.int32)
    allowed = (position[None, :] <= position[:, None]) & (position[None, :] < seq_length)
    q_heads = queries.reshape(tok_rows, KEY_VALUE_HEADS, group_size, HEAD_DIM)
    k_heads = keys.reshape(tok_rows, KEY_VALUE_HEADS, HEAD_DIM)
    v_heads = value_outputs.reshape(tok_rows, KEY_VALUE_HEADS, HEAD_DIM)
    scores = jnp.einsum(
        "tkgd,skd->kgts", q_heads, k_heads, preferred_element_type=jnp.float32
    ) / math.sqrt(HEAD_DIM)
    scores = jnp.where(allowed, scores, masked_score)
    row_max = jnp.max(scores, axis=-1, keepdims=True)
    weights = jnp.exp(scores - row_max)
    attn_probs = (weights / jnp.sum(weights, axis=-1, keepdims=True)).astype(jnp.bfloat16)
    output = jnp.einsum(
        "kgts,skd->tkgd", attn_probs, v_heads, preferred_element_type=jnp.float32
    ).reshape(tok_rows, HEADS * HEAD_DIM)
    live_rows = (position < seq_length)[:, None]
    differ = jnp.where(live_rows, output - target.astype(jnp.float32), 0.0)
    loss_local = jnp.sum(differ * differ)
    cotangent = differ.astype(jnp.bfloat16).reshape(tok_rows, KEY_VALUE_HEADS, group_size, HEAD_DIM)
    value_grad = jnp.einsum(
        "kgts,tkgd->skd", attn_probs, cotangent, preferred_element_type=jnp.float32
    )
    value_grad = value_grad.reshape(tok_rows, KEY_VALUE_HEADS * HEAD_DIM).astype(jnp.bfloat16)
    latent_grad = lax.dot_general(
        value_grad, up_factor_slice, (((1,), (1,)), ((), ())), preferred_element_type=jnp.float32
    ).astype(jnp.bfloat16)
    up_term = lax.dot_general(
        adapter_hidden, value_grad, (((0,), (0,)), ((), ())), preferred_element_type=jnp.float32
    )
    count_local = seq_length.astype(jnp.float32)
    columns = hidden
    down_map_gradient = lax.psum(
        adapter_scale
        * lax.dot_general(
            columns, latent_grad, (((0,), (0,)), ((), ())), preferred_element_type=jnp.float32
        ),
        "dp",
    )
    down_map_gradient = lax.psum_scatter(down_map_gradient, "fsdp", scatter_dimension=0, tiled=True)
    up_map_gradient, loss_sum, token_grand_count = lax.psum(
        (adapter_scale * up_term, loss_local, count_local), ("dp", "fsdp")
    )
    up_map_gradient = up_map_gradient / token_grand_count
    down_map_gradient = down_map_gradient / token_grand_count
    loss = loss_sum / (2.0 * token_grand_count)
    average_down_next = average_decay * average_down_map + (1.0 - average_decay) * (
        adapter_down_map - learning_rate * down_map_gradient
    )
    average_up_next = average_decay * average_up_map + (1.0 - average_decay) * (
        adapter_up_map - learning_rate * up_map_gradient
    )
    return (down_map_gradient, up_map_gradient, average_down_next, average_up_next, loss)


def solution(mesh):
    placed = (
        P(("dp", "fsdp"), None),
        P(("dp", "fsdp"), None),
        P(("dp", "fsdp"), None),
        P(("dp", "fsdp"), None),
        P(("dp", "fsdp")),
        P("fsdp", None),
        P("fsdp", None),
        P(),
        P("fsdp", None),
        P(),
    )
    return jax.shard_map(
        per_device,
        mesh=mesh,
        in_specs=placed,
        out_specs=(P("fsdp", None), P(), P("fsdp", None), P(), P()),
        check_vma=False,
    )
```

profile of v0, /device:TPU:0, one launch (start us, length us, event | category | flops | bytes accessed | tf_op | source)
XLA Modules:
  0.0 281.5 jit_solution(8382225691264275477)
XLA Ops:
  7.2 0.0 copy-start
  7.2 0.0 copy-start.3
  7.2 0.0 all-gather.2.cloned.1.call-start
  7.2 0.7 all-gather.2.cloned.1.call-update
  7.9 0.0 reduce-scatter.2.cloned.1.call-start
  8.6 1.8 reshape.40
  10.4 1.0 reshape.39
  11.4 0.0 copy-done.3
  11.5 11.3 %all_gather.7 = bf16[4096,64]{0,1:T(8,128)(2,1)S(1)} all-gather(bf16[512,64]{0,1:T(8,128)(2,1)S(1)} %convert_element_type.36), channel_id=1, replica_groups=mesh['dp'=4,'fsdp'=8] {'fsdp'}, dimensions={0}, use_global_device_ids=true | all-gather | bytes 589824 | tf_op jit(solution)/shard_map/all_gather | solution.py:44
  22.8 0.1 fusion.13
  22.9 0.0 copy-done
  22.9 1.4 convolution_convert_fusion.1
  24.3 0.7 fusion.10
  25.0 1.2 fusion.19
  26.3 1.8 divide_convert_fusion
  28.0 0.0 copy-start.1
  28.0 0.0 copy-start.5
  28.0 21.2 %all-gather.2.cloned.1.call-done = bf16[4096,512]{1,0:T(8,128)(2,1)} async-done(((bf16[512,512]{1,0:T(8,128)(2,1)}), bf16[4096,512]{1,0:T(8,128)(2,1)}) %all-gather.2.cloned.1.call-update) | async-done | bytes 4194320 | tf_op jit(solution)/shard_map/all_gather | solution.py:39
  49.2 3.4 %fusion.20 = f32[256,512]{1,0:T(8,128)S(1)} fusion(bf16[256,4096]{1,0:T(8,128)(2,1)S(1)} %copy-done, bf16[4096,512]{1,0:T(8,128)(2,1)} %all-gather.2.cloned.1.call-done), kind=kOutput, calls=%fused_computation.36 | convolution fusion | flops 1073741824 | bytes 6815744 | tf_op jit(solution)/shard_map/dot_general | solution.py:37
  52.7 0.0 copy-done.1
  52.7 0.0 copy-done.5
  52.7 0.3 fusion.8
  52.9 0.1 copy.27
  53.1 3.3 %fusion.21 = f32[4,128,4,256]{3,1,2,0:T(8,128)} fusion(bf16[256,4,128,1]{0,2,3,1:T(8,128)(2,1)S(1)} %bitcast.51, bf16[4,4,256,256]{2,3,1,0:T(8,128)(2,1)} %divide_convert_fusion), kind=kOutput, calls=%fused_computation.37 | convolution fusion | flops 268435456 | bytes 4456448 | tf_op jit(solution)/shard_map/kgts,skd->tkgd/dot_general | solution.py:65
  56.4 0.0 copy-start.2
  56.4 3.0 %copy.19 = f32[256,2048]{1,0:T(8,128)} copy(f32[256,2048]{0,1:T(8,128)} %bitcast.47) | data formatting | bytes 4194304 | tf_op jit(solution)/shard_map/reshape | solution.py:67
  59.5 0.0 copy-done.2
  59.5 3.6 %multiply_reduce_fusion = (f32[]{:T(128)}, bf16[256,2048]{1,0:T(8,128)(2,1)}) fusion(f32[256,2048]{1,0:T(8,128)} %copy.19, bf16[256,2048]{1,0:T(8,128)(2,1)S(1)} %copy-done.2, pred[256]{0:T(512)(128)(4,1)S(1)} %iota_compare_fusion.1), kind=kLoop, calls=%fused_computation.7 | loop fusion | flops 3145727 | bytes 4194564 | tf_op jit(solution)/shard_map/reduce_sum | solution.py:70
  63.1 1.5 copy.30
  64.6 2.4 fusion.9
  67.0 0.0 copy-start.6
  67.0 0.0 copy-start.7
  67.0 0.0 copy-start.4
  67.0 0.0 copy-start.8
  67.0 1.8 fusion.1
  68.9 0.0 reduce-scatter.2.cloned.1.call-update
  68.9 0.0 all-reduce.4.cloned.1.call-start
  68.9 0.0 copy-done.6
  69.0 0.9 convolution_multiply_fusion.2
  69.8 0.0 all-reduce.4.cloned.1.call-update
  69.8 0.0 all-reduce.6.cloned.1.call-start
  69.9 39.5 %all-reduce = (f32[]{:T(128)}, f32[]{:T(128)}) all-reduce(f32[]{:T(128)S(6)} %convert_element_type.47, f32[]{:T(128)} %get-tuple-element.11), channel_id=1, replica_groups=mesh['dp'=4,'fsdp'=8] {'dp','fsdp'}, use_global_device_ids=true, to_apply=%region_4.5 | all-reduce | flops 2 | bytes 16 | tf_op jit(solution)/shard_map/psum | solution.py:92
  110.7 0.0 reduce-scatter.2.cloned.1.call-done
  110.7 0.0 all-reduce.6.cloned.1.call-update
  110.7 125.1 %all-reduce.4.cloned.1.call-done = f32[64,512]{1,0:T(8,128)} async-done(((f32[64,512]{1,0:T(8,128)}), f32[64,512]{1,0:T(8,128)}) %all-reduce.4.cloned.1.call-update) | async-done | bytes 131088 | tf_op jit(solution)/shard_map/psum | solution.py:92
  235.8 0.0 copy-done.7
  235.8 2.2 multiply_add_fusion
  238.0 33.7 %all-reduce.6.cloned.1.call-done = f32[512,64]{0,1:T(8,128)} async-done(((f32[512,64]{0,1:T(8,128)}), f32[512,64]{0,1:T(8,128)}) %all-reduce.6.cloned.1.call-update) | async-done | bytes 131088 | tf_op jit(solution)/shard_map/psum | solution.py:84
  271.7 0.0 copy-done.4
  271.7 0.0 copy-done.8
  271.7 2.2 multiply_add_fusion.1
  (2 shorter events, 0.0 us)
Async XLA Ops:
  7.2 15.8 %copy-start = (bf16[256,4096]{1,0:T(8,128)(2,1)S(1)}, bf16[256,4096]{1,0:T(8,128)(2,1)}, u32[]{:S(2)}) copy-start(bf16[256,4096]{1,0:T(8,128)(2,1)} %param.10) | copy-start | bytes 6291460
  7.2 4.3 %copy-start.3 = (f32[512,64]{0,1:T(8,128)S(1)}, f32[512,64]{0,1:T(8,128)}, u32[]{:S(2)}) copy-start(f32[512,64]{0,1:T(8,128)} %param.16) | copy-start | bytes 393220
  7.2 42.0 %all-gather.2.cloned.1.call-start = ((), (), s32[]{:S(2)}) async-start(), calls=%async_computation.1 | async-start | bytes 4718592 | tf_op jit(solution)/shard_map/all_gather | solution.py:39
  7.9 102.8 %reduce-scatter.2.cloned.1.call-start = ((), (), s32[]{:S(2)}) async-start(), calls=%async_computation.3 | async-start | bytes 1179648 | tf_op jit(solution)/shard_map/reduce_scatter | solution.py:91
  28.0 24.6 %copy-start.1 = (f32[64,512]{1,0:T(8,128)S(1)}, f32[64,512]{1,0:T(8,128)}, u32[]{:S(2)}) copy-start(f32[64,512]{1,0:T(8,128)} %param.17) | copy-start | bytes 393220
  28.0 24.6 %copy-start.5 = (bf16[256,64]{0,1:T(8,128)(2,1)S(1)}, bf16[256,64]{0,1:T(8,128)(2,1)}, u32[]{:S(2)}) copy-start(bf16[256,64]{0,1:T(8,128)(2,1)} %convolution_convert_fusion.1) | copy-start | bytes 98308
  56.4 3.0 %copy-start.2 = (bf16[256,2048]{1,0:T(8,128)(2,1)S(1)}, bf16[256,2048]{1,0:T(8,128)(2,1)}, u32[]{:S(2)}) copy-start(bf16[256,2048]{1,0:T(8,128)(2,1)} %param.13) | copy-start | bytes 3145732
  67.0 2.0 copy-start.6
  67.0 168.8 %copy-start.7 = (f32[64,512]{1,0:T(8,128)S(1)}, f32[64,512]{1,0:T(8,128)}, u32[]{:S(2)}) copy-start(f32[64,512]{1,0:T(8,128)} %param.19) | copy-start | bytes 393220
  67.0 204.7 %copy-start.4 = (f32[512,64]{0,1:T(8,128)S(1)}, f32[512,64]{0,1:T(8,128)}, u32[]{:S(2)}) copy-start(f32[512,64]{0,1:T(8,128)} %param.16) | copy-start | bytes 393220
  67.0 204.7 %copy-start.8 = (f32[512,64]{0,1:T(8,128)S(1)}, f32[512,64]{0,1:T(8,128)}, u32[]{:S(2)}) copy-start(f32[512,64]{0,1:T(8,128)} %param.18) | copy-start | bytes 393220
  68.9 166.9 %all-reduce.4.cloned.1.call-start = ((), (), s32[]{:S(2)}) async-start(), calls=%async_computation.2 | async-start | bytes 262144 | tf_op jit(solution)/shard_map/psum | solution.py:92
  69.8 201.8 %all-reduce.6.cloned.1.call-start = ((), (), s32[]{:S(2)}) async-start(), calls=%async_computation.4 | async-start | bytes 262144 | tf_op jit(solution)/shard_map/psum | solution.py:84
Sparse Core Ops, SparseCore 0:
  9.9 39.2 all-gather.1
  69.0 35.9 reduce-scatter.1
  111.1 124.5 all-reduce.3
  237.9 33.6 all-reduce.5
where the time goes:
time: 282 us
  waiting for transfers between devices  181 us (64%)
  blocking collectives  50.9 us (18%)
  between operations  16.9 us (6%)
  matrix products  14.2 us (5%)
  other arithmetic  11.1 us (4%)
  local copies, waits for them, and re-layouts  7.48 us (3%)
    psum x1, waiting for transfers between devices, per_device(): lax.psum((adapter_scale * up_term, loss_local, count_local), ('dp', 'fsdp'))  125 us
    psum x1, blocking collectives, per_device(): lax.psum((adapter_scale * up_term, loss_local, count_local), ('dp', 'fsdp'))  39.5 us
    psum x1, waiting for transfers between devices, per_device(): lax.psum(adapter_scale * lax.dot_general(columns, latent_grad, (((0,), (0...  33.7 us
    all_gather x1, waiting for transfers between devices, per_device(): lax.all_gather(value_weight_frozen, 'fsdp', axis=0, tiled=True)  21.2 us
    all_gather x1, blocking collectives, per_device(): lax.all_gather(down_factor_slice, 'fsdp', axis=0, tiled=True)  11.3 us
  transfers between devices with their start and end apart: 4, of which 3 were waited for; matrix products, arithmetic and copies ran while one was open for 4% of the time, Pallas kernels for 0%

commit v1 on v0

v1 whole, which is shorter than its diff:
```python
import functools
import math

import jax
import jax.numpy as jnp
from jax import lax
from jax.experimental import pallas as pl
from jax.experimental.pallas import tpu as pltpu
from jax.sharding import PartitionSpec as P

HEADS = 16
KEY_VALUE_HEADS = 4
HEAD_DIM = 128
GROUP = HEADS // KEY_VALUE_HEADS

adapter_scale = 2.0
average_decay = 0.9
learning_rate = 1.0
masked_score = -1e30
f32 = jnp.float32
bf16 = jnp.bfloat16


def dot(a, b, dims=((1,), (0,))):
    return lax.dot_general(a, b, (dims, ((), ())), preferred_element_type=f32)


def kernel(
    ndp, nf,
    hid_hbm, q_hbm, k_hbm, tgt_hbm, len_ref, w_hbm, down_ref, up_ref, avd_ref, avu_ref,
    gd_ref, gu_ref, nd_ref, nu_ref, loss_ref,
    hid, qv, kv, tgt, wall, dall, acc, lat, probs, probs_t, cot, vg,
    dpart, dfrom, upart, ufrom, spart, sfrom,
    send2, got2, sc2, send3, got3, sc3, uhalf, uother,
    lsem, g_ss, g_rs, p_ss, p_rs, a_ss, a_rs, b_ss, b_rs, c_ss, c_rs, e_ss, e_rs,
):
    z = lax.axis_index("dp")
    me = lax.axis_index("fsdp")
    chip, core = me // 2, me % 2
    nch = nf // 2
    rows = w_hbm.shape[0]
    rank = up_ref.shape[0]
    width = up_ref.shape[1]
    half = width // 2
    toks = hid.shape[0]
    xor = nch & (nch - 1) == 0

    def toward(d):
        return chip ^ d if xor else lax.rem(chip + d, nch)

    def origin(d):
        return chip ^ d if xor else lax.rem(chip + nch - d, nch)

    def remote(src, dst, ss, rs, fsdp=None, dp=None):
        where = {"fsdp": me if fsdp is None else fsdp, "dp": z if dp is None else dp}
        return pltpu.make_async_remote_copy(
            src_ref=src, dst_ref=dst, send_sem=ss, recv_sem=rs,
            device_id=where, device_id_type=pl.DeviceIdType.MESH,
        )

    partner = 2 * chip + 1 - core

    def rows_of(i):
        return pl.ds(pl.multiple_of(i * rows, rows), rows)

    loads = [
        pltpu.make_async_copy(w_hbm, wall.at[rows_of(me)], lsem.at[0]),
        pltpu.make_async_copy(k_hbm, kv, lsem.at[1]),
        pltpu.make_async_copy(q_hbm, qv, lsem.at[2]),
        pltpu.make_async_copy(hid_hbm, hid, lsem.at[3]),
        pltpu.make_async_copy(tgt_hbm, tgt, lsem.at[4]),
    ]
    for c in loads:
        c.start()

    barrier = pltpu.get_barrier_semaphore()
    pl.semaphore_signal(barrier, inc=1, device_id={"fsdp": partner, "dp": z}, device_id_type=pl.DeviceIdType.MESH)
    for d in range(1, nch):
        pl.semaphore_signal(barrier, inc=1, device_id={"fsdp": 2 * toward(d) + core, "dp": z}, device_id_type=pl.DeviceIdType.MESH)
    for d in range(1, ndp):
        pl.semaphore_signal(barrier, inc=1, device_id={"fsdp": me, "dp": lax.rem(z + d, ndp)}, device_id_type=pl.DeviceIdType.MESH)
    dall[me] = down_ref[...].T.astype(bf16)
    loads[0].wait()
    pl.semaphore_wait(barrier, 1 + (nch - 1) + (ndp - 1))

    sends = []

    def both(i, ss, rs, to):
        out = [
            remote(wall.at[rows_of(i)], wall.at[rows_of(i)], ss.at[0], rs.at[0], fsdp=to),
            remote(dall.at[i], dall.at[i], ss.at[1], rs.at[1], fsdp=to),
        ]
        for c in out:
            c.start()
        sends.extend(out)
        return out

    direct = {d: both(me, g_ss.at[d], g_rs.at[d], 2 * toward(d) + core) for d in range(1, nch)}
    relay = {0: both(me, p_ss.at[0], p_rs.at[0], partner)}

    seq_length = len_ref[0]
    key_at = lax.broadcasted_iota(jnp.int32, (toks, toks), 1)
    query_at = lax.broadcasted_iota(jnp.int32, (toks, toks), 0)
    allowed = (key_at <= query_at) & (key_at < seq_length)
    scale = 1.0 / math.sqrt(HEAD_DIM)
    loads[1].wait()
    loads[2].wait()
    for h in range(HEADS):
        g = h // GROUP
        s = dot(qv[:, h * HEAD_DIM:(h + 1) * HEAD_DIM], kv[:, g * HEAD_DIM:(g + 1) * HEAD_DIM], ((1,), (1,)))
        s = jnp.where(allowed, s, masked_score)
        w = jnp.exp((s - jnp.max(s, axis=1, keepdims=True)) * scale)
        p = (w / jnp.sum(w, axis=1, keepdims=True)).astype(bf16)
        probs[h] = p
        probs_t[h] = p.T
    loads[3].wait()
    loads[4].wait()

    aligned = rows % 128 == 0
    acc[...] = jnp.zeros_like(acc)
    lat[...] = jnp.zeros_like(lat)

    def piece(i, static=False):
        if static:
            x = hid[:, i * rows:(i + 1) * rows]
        else:
            x = hid[:, pl.ds(pl.multiple_of(i * rows, rows), rows)]
        acc[...] += dot(x, wall[rows_of(i), :] if not static else wall[i * rows:(i + 1) * rows, :])
        lat[...] += dot(x, dall[i], ((1,), (1,)))

    if aligned:
        piece(me)
    for d in range(1, nch):
        for c in direct[d]:
            c.wait_recv()
        i = 2 * origin(d) + core
        relay[d] = both(i, p_ss.at[d], p_rs.at[d], partner)
        for c in relay[d - 1]:
            c.wait_recv()
        if aligned:
            piece(i)
            piece(2 * origin(d - 1) + 1 - core)
    for c in relay[nch - 1]:
        c.wait_recv()
    if aligned:
        piece(2 * origin(nch - 1) + 1 - core)
    else:
        for i in range(nf):
            piece(i, True)

    up = up_ref[...].astype(bf16)
    latent = lat[...].astype(bf16)
    values = (acc[...] + adapter_scale * dot(latent, up)).astype(bf16)
    live = lax.broadcasted_iota(jnp.int32, (toks, 1), 0) < seq_length
    total = jnp.zeros((toks, HEAD_DIM), f32)
    for g in range(KEY_VALUE_HEADS):
        v = values[:, g * HEAD_DIM:(g + 1) * HEAD_DIM]
        grad = jnp.zeros((toks, HEAD_DIM), f32)
        for j in range(GROUP):
            h = g * GROUP + j
            differ = dot(probs[h], v) - tgt[:, h * HEAD_DIM:(h + 1) * HEAD_DIM].astype(f32)
            differ = jnp.where(live, differ, 0.0)
            total += differ * differ
            grad += dot(probs_t[h], differ.astype(bf16))
        vg[:, g * HEAD_DIM:(g + 1) * HEAD_DIM] = grad.astype(bf16)
    value_grad = vg[...]
    u = dot(lat[...].T.astype(bf16), value_grad)
    upart[0] = u[:, :half]
    upart[1] = u[:, half:]
    loss_local = jnp.sum(jnp.sum(total, axis=0, keepdims=True), axis=1, keepdims=True)
    count_local = jnp.sum(live.astype(f32), axis=0, keepdims=True)
    row = lax.broadcasted_iota(jnp.int32, spart.shape, 0)
    spart[...] = jnp.where(row == 0, loss_local, count_local)
    lg = dot(up, value_grad, ((1,), (1,))).astype(bf16)
    for i in range(nf):
        dpart[i % 2, i // 2] = dot(lg, hid[:, i * rows:(i + 1) * rows])

    step = [
        remote(dpart.at[1 - core], dfrom, a_ss.at[0], a_rs.at[0], fsdp=partner),
        remote(upart.at[1 - core], ufrom, a_ss.at[1], a_rs.at[1], fsdp=partner),
        remote(spart, sfrom, a_ss.at[2], a_rs.at[2], fsdp=partner),
    ]
    for c in step:
        c.start()
    for c in step:
        c.wait_recv()
    sends.extend(step)
    usum = (upart[core] + ufrom[...]).astype(bf16)
    for q in range(nch):
        send2[q, :, :rows] = (dpart[core, q] + dfrom[q]).astype(bf16)
        send2[q, :, rows:] = usum
    sc2[chip] = spart[...] + sfrom[...]
    got2[chip] = send2[chip]

    step = []
    for d in range(1, nch):
        to = toward(d)
        step.append(remote(send2.at[to], got2.at[chip], b_ss.at[d, 0], b_rs.at[d, 0], fsdp=2 * to + core))
        step.append(remote(sc2.at[chip], sc2.at[chip], b_ss.at[d, 1], b_rs.at[d, 1], fsdp=2 * to + core))
    for c in step:
        c.start()
    for c in step:
        c.wait_recv()
    sends.extend(step)
    t = got2[0].astype(f32)
    s = sc2[0]
    for q in range(1, nch):
        t += got2[q].astype(f32)
        s += sc2[q]
    got3[z] = t.astype(bf16)
    sc3[z] = s

    step = []
    for d in range(1, ndp):
        to = lax.rem(z + d, ndp)
        step.append(remote(got3.at[z], got3.at[z], c_ss.at[d, 0], c_rs.at[d, 0], dp=to))
        step.append(remote(sc3.at[z], sc3.at[z], c_ss.at[d, 1], c_rs.at[d, 1], dp=to))
    for c in step:
        c.start()
    for c in step:
        c.wait_recv()
    sends.extend(step)
    t = got3[0].astype(f32)
    s = sc3[0]
    for q in range(1, ndp):
        t += got3[q].astype(f32)
        s += sc3[q]
    uhalf[...] = t[:, rows:]
    last = remote(uhalf, uother, e_ss, e_rs, fsdp=partner)
    last.start()
    count = s[1:2, 0:1]
    factor = adapter_scale / count
    loss_ref[...] = s[0:1, 0:1] / (2.0 * count)
    gd = (t[:, :rows] * factor).T
    gd_ref[...] = gd
    nd_ref[...] = average_decay * avd_ref[...] + (1.0 - average_decay) * (down_ref[...] - learning_rate * gd)
    last.wait_recv()
    mine, other = uhalf[...], uother[...]
    first = core == 0
    gu = jnp.concatenate([jnp.where(first, mine, other), jnp.where(first, other, mine)], axis=1) * factor
    gu_ref[...] = gu
    nu_ref[...] = average_decay * avu_ref[...] + (1.0 - average_decay) * (up_ref[...] - learning_rate * gu)
    sends.append(last)
    for c in sends:
        c.wait_send()


def per_device(
    ndp, nf,
    hidden, queries, keys, target, lengths,
    value_weight_frozen, adapter_down_map, adapter_up_map, average_down_map, average_up_map,
):
    toks, dim = hidden.shape
    rows, width = value_weight_frozen.shape
    rank = adapter_up_map.shape[0]
    nch = nf // 2
    half = width // 2
    vm = pl.BlockSpec(memory_space=pltpu.VMEM)
    anyspace = pl.BlockSpec(memory_space=pl.ANY)
    shape = jax.ShapeDtypeStruct
    dma = pltpu.SemaphoreType.DMA
    out = pl.pallas_call(
        functools.partial(kernel, ndp, nf),
        out_shape=(
            shape((rows, rank), f32), shape((rank, width), f32),
            shape((rows, rank), f32), shape((rank, width), f32), shape((1, 1), f32),
        ),
        in_specs=[anyspace] * 4 + [pl.BlockSpec(memory_space=pltpu.SMEM), anyspace] + [vm] * 4,
        out_specs=(vm,) * 5,
        scratch_shapes=[
            pltpu.VMEM(hidden.shape, bf16),
            pltpu.VMEM(queries.shape, bf16),
            pltpu.VMEM(keys.shape, bf16),
            pltpu.VMEM(target.shape, bf16),
            pltpu.VMEM((dim, width), bf16),
            pltpu.VMEM((nf, rank, rows), bf16),
            pltpu.VMEM((toks, width), f32),
            pltpu.VMEM((toks, rank), f32),
            pltpu.VMEM((HEADS, toks, toks), bf16),
            pltpu.VMEM((HEADS, toks, toks), bf16),
            pltpu.VMEM((toks, HEAD_DIM), bf16),
            pltpu.VMEM((toks, width), bf16),
            pltpu.VMEM((2, nch, rank, rows), f32),
            pltpu.VMEM((nch, rank, rows), f32),
            pltpu.VMEM((2, rank, half), f32),
            pltpu.VMEM((rank, half), f32),
            pltpu.VMEM((8, 128), f32),
            pltpu.VMEM((8, 128), f32),
            pltpu.VMEM((nch, rank, rows + half), bf16),
            pltpu.VMEM((nch, rank, rows + half), bf16),
            pltpu.VMEM((nch, 8, 128), f32),
            pltpu.VMEM((nch, rank, rows + half), bf16),
            pltpu.VMEM((ndp, rank, rows + half), bf16),
            pltpu.VMEM((ndp, 8, 128), f32),
            pltpu.VMEM((rank, half), f32),
            pltpu.VMEM((rank, half), f32),
            dma((5,)),
            dma((nch, 2)), dma((nch, 2)),
            dma((nch, 2)), dma((nch, 2)),
            dma((3,)), dma((3,)),
            dma((nch, 2)), dma((nch, 2)),
            dma((ndp, 2)), dma((ndp, 2)),
            dma, dma,
        ],
        compiler_params=pltpu.CompilerParams(
            collective_id=0, has_side_effects=True, vmem_limit_bytes=60 * 1024 * 1024
        ),
    )(
        hidden, queries, keys, target, lengths,
        value_weight_frozen, adapter_down_map, adapter_up_map, average_down_map, average_up_map,
    )
    return out[0], out[1], out[2], out[3], out[4].reshape(())


def solution(mesh):
    both = P(("dp", "fsdp"), None)
    placed = (
        both, both, both, both, P(("dp", "fsdp")),
        P("fsdp", None), P("fsdp", None), P(), P("fsdp", None), P(),
    )
    return jax.shard_map(
        functools.partial(per_device, mesh.shape["dp"], mesh.shape["fsdp"]),
        mesh=mesh,
        in_specs=placed,
        out_specs=(P("fsdp", None), P(), P("fsdp", None), P(), P()),
        check_vma=False,
    )
```

time: 282 us -> 70.5 us (0.25)
  waiting for transfers between devices: 181 us -> 0 us
  Pallas kernels: 0 us -> 57.1 us
  blocking collectives: 50.9 us -> 0 us
  matrix products: 14.2 us -> 0 us
  between operations: 16.9 us -> 3.04 us
  other arithmetic: 11.1 us -> 0 us
    psum x2 -> x0, waiting for transfers between devices: 159 us -> none  [the longest x1 125 us: per_device(): lax.psum((adapter_scale * up_term, loss_local, count_local), ('dp', 'fsdp'))]
    pallas_call x0 -> x1, Pallas kernels: none -> 57.1 us  [per_device(): pl.pallas_call(functools.partial(kernel, ndp, nf), out_shape=(shape((rows...]
    psum x1 -> x0, blocking collectives: 39.5 us -> none  [per_device(): lax.psum((adapter_scale * up_term, loss_local, count_local), ('dp', 'fsdp'))]
    all_gather x1 -> x0, waiting for transfers between devices: 21.2 us -> none  [per_device(): lax.all_gather(value_weight_frozen, 'fsdp', axis=0, tiled=True)]
    dot_general x8 -> x0, matrix products: 14.2 us -> none  [the longest x1 3.42 us: per_device(): jnp.dot(columns, lax.all_gather(value_weight_frozen, 'fsdp', axis=0, tile...]
    all_gather x1 -> x0, blocking collectives: 11.3 us -> none  [per_device(): lax.all_gather(down_factor_slice, 'fsdp', axis=0, tiled=True)]
    unnamed x18 -> x6, local copies, waits for them, and re-layouts: 0.05 us -> 10 us
    reshape x5 -> x0, local copies, waits for them, and re-layouts: 7.43 us -> none  [the longest x1 3.02 us: per_device(): output = jnp.einsum('kgts,skd->tkgd', attn_probs, v_heads, preferred_elem...]
  transfers between devices with their start and end apart: 4 -> 0, of which waited for: 3 -> 0; matrix products, arithmetic and copies ran while one was open for 4% -> 0% of each run, Pallas kernels for 0% -> 0%
where the time goes in v1:
time: 70.5 us; the launch traced here: 70.2 us
  Pallas kernels  57.1 us (81%)
  local copies, waits for them, and re-layouts  10 us (14%)
  between operations  3.04 us (4%)
    pallas_call x1, Pallas kernels, per_device(): pl.pallas_call(functools.partial(kernel, ndp, nf), out_shape=(shape((rows...  57.1 us
    unnamed x6, local copies, waits for them, and re-layouts  10 us

profile of v1, /device:TPU:0, one launch (start us, length us, event | category | flops | bytes accessed | tf_op | source)
XLA Modules:
  0.0 70.2 jit_solution(10192136828651519371)
XLA Ops:
  1.3 1.7 %copy.15.down_ref = f32[512,64]{1,0:T(8,128)} copy(f32[512,64]{0,1:T(8,128)} %param.16) | data formatting | bytes 262144 | tf_op args[6]
  3.0 1.7 %copy.16.avd_ref = f32[512,64]{1,0:T(8,128)} copy(f32[512,64]{0,1:T(8,128)} %param.18) | data formatting | bytes 262144 | tf_op args[8]
  4.7 57.1 %shard_map.137 = (f32[512,64]{1,0:T(8,128)}, f32[64,512]{1,0:T(8,128)}, f32[512,64]{1,0:T(8,128)}, f32[64,512]{1,0:T(8,128)}, f32[1,1]{1,0:T(1,128)}) custom-call(bf16[256,4096]{1,0:T(8,128)(2,1)} %hid_hbm.1, bf16[256,2048]{1,0:T(8,128)(2,1)} %q_hbm.1, bf16[256,512]{1,0:T(8,128)(2,1)} %k_hbm.1, bf16[256,2048]{1,0:T(8,128)(2,1)} %tgt_hbm.1, ...), custom_call_target="tpu_custom_call" | custom-call | tf_op jit(solution)/shard_map/pallas_call | solution.py:262
  61.9 1.7 %copy.17 = f32[512,64]{0,1:T(8,128)} copy(f32[512,64]{1,0:T(8,128)} %get-tuple-element.15) | data formatting | bytes 262144
  63.6 1.7 %copy.18 = f32[512,64]{0,1:T(8,128)} copy(f32[512,64]{1,0:T(8,128)} %get-tuple-element.17) | data formatting | bytes 262144
  65.3 1.6 %copy.23 = f32[64,512]{1,0:T(8,128)} copy(f32[64,512]{1,0:T(8,128)} %get-tuple-element.26) | data formatting | bytes 262144
  66.9 1.6 %copy.24 = f32[64,512]{1,0:T(8,128)} copy(f32[64,512]{1,0:T(8,128)} %get-tuple-element.28) | data formatting | bytes 262144
